TPU v7x, 128 devices: a whole 4x4x4 slice. The times are simulated.
128 devices in a mesh: ep: 32 (over y, z, core), dp: 4 (over x).
Axes of the slice: x: 4, y: 4, z: 4, core: 2. Of those that a mesh axis runs over, the one named last changes fastest.
Arguments:
- lengths: int32 [128, 16], P(('ep', 'dp')), may hold values from 1 to 512, as said below
- id_lists: int32 [128, 16, 512], P(('ep', 'dp')), may hold values from 0 to 65535, as said below
- feature_slots: int32 [16], replicated, may hold values from 0 to 15, each once
- embedding_table: bfloat16 [1048576, 128], P(('ep', 'dp')), may hold values from -6 to 6
Outputs:
- embedded: bfloat16 [128, 16, 512, 128], P(('ep', 'dp'))
Inputs may be any that keep to these rules, and one draw needn't show every extreme that they name: `lengths`: every user has some feature whose length is exactly 512. `id_lists`: among the valid entries (positions below the list's length) of the 1 users of one device, at most 80 ids lie in any one block of 512 ids that starts at a multiple of 512; in every draw some block holds exactly 80 valid ids from every device. Entries past a list's length hold arbitrary ids of the range.
All inputs are finite; a program needn't handle non-finite values.
Results may differ from a plain program's by a relative error of at most 0.001.
Values may be sent and summed in bfloat16 or wider, within the bound.
No kernel may reach another device: no remote copies, remote signals or barrier semaphores. Data moves between devices by JAX's collectives and lax.ppermute only.
A program may use at most 64 MiB of HBM per device.

v0:
```python
import functools

import jax
import jax.numpy as jnp
from jax import lax
from jax.experimental import pallas as pl
from jax.experimental.pallas import tpu as pltpu
from jax.sharding import PartitionSpec as P

LANES = 128
BLOCK = 256
GROUP = 16
WINDOW = 128
PAD = 8
DEPTH = 2
LINES = 16
MIB = 2**20


def rank_kernel(
    per_owner,
    capacity,
    len_hbm,
    slot_hbm,
    ids_hbm,
    tab_hbm,
    req_ref,
    tgt_ref,
    tab_ref,
    len_ref,
    slot_ref,
    ids_ref,
    sems,
):
    copies = [
        pltpu.make_async_copy(src, dst, sems.at[k])
        for k, (src, dst) in enumerate(
            [(len_hbm, len_ref), (slot_hbm, slot_ref), (ids_hbm, ids_ref), (tab_hbm, tab_ref)]
        )
    ]
    for copy in copies:
        copy.start()
    feats, span = ids_ref.shape
    owners = req_ref.shape[0]
    half = jnp.bfloat16
    one, zero = jnp.ones((16, BLOCK), half), jnp.zeros((16, BLOCK), half)
    row_of = lax.broadcasted_iota(jnp.int32, (16, BLOCK), 0).astype(jnp.float32)
    owner_rows = [(row_of + 16 * t).astype(half) for t in range(owners // 16)]
    rank_rows = [(row_of + (16 * t + 1)).astype(half) for t in range(capacity // 16)]
    earlier = lax.broadcasted_iota(jnp.int32, (BLOCK, BLOCK), 0)
    later = lax.broadcasted_iota(jnp.int32, (BLOCK, BLOCK), 1)
    up_to = jnp.where(earlier <= later, 1.0, 0.0).astype(half)
    lane = lax.broadcasted_iota(jnp.int32, (1, BLOCK), 1)
    for copy in copies[:3]:
        copy.wait()
    ids = ids_ref[...]
    owner = ids >> (per_owner.bit_length() - 1)
    base = (owner * capacity - 1).astype(jnp.float32)
    owner = owner.astype(jnp.float32)
    row = (ids & (per_owner - 1)) * feats
    low = (128 + (row & 127)).astype(jnp.float32)
    high = jnp.exp2((row >> 7).astype(jnp.float32))

    offset = [jnp.zeros((16, LANES), half) for _ in owner_rows]
    request = jnp.zeros((owners, capacity), jnp.float32)
    per_feature = span // BLOCK

    def spread(x):
        return jnp.broadcast_to(x, (16, BLOCK)).astype(half)

    for step in range(feats * per_feature):
        f, at = step // per_feature, step % per_feature * BLOCK

        def line(x):
            return x[f : f + 1, at : at + BLOCK]

        valid = (lane + at) < len_ref[0, f]
        key = spread(jnp.where(valid, line(owner), -1.0))
        hot = [jnp.where(rows == key, one, zero) for rows in owner_rows]
        hot_all = jnp.concatenate(hot, axis=0)
        counted = jnp.dot(hot_all, up_to, preferred_element_type=jnp.float32)
        total = jnp.broadcast_to(counted[:, BLOCK - 1 :], (owners, LANES)).astype(half)
        counted = counted.astype(half)
        picked = zero
        for t in range(len(hot)):
            at_t = slice(16 * t, 16 * t + 16)
            before = counted[at_t] + jnp.concatenate([offset[t]] * (BLOCK // LANES), axis=1)
            picked = picked + hot[t] * before
            offset[t] = offset[t] + total[at_t]
        rank = jnp.sum(picked.astype(jnp.float32), axis=0, keepdims=True)
        key = spread(rank)
        code = spread((line(low) + slot_ref[f].astype(jnp.float32)) * line(high))
        request = request + lax.dot_general(
            hot_all,
            jnp.concatenate([jnp.where(rows == key, code, zero) for rows in rank_rows], axis=0),
            (((1,), (1,)), ((), ())),
            preferred_element_type=jnp.float32,
        )
        place = jnp.where(valid, line(base) + rank, float(owners * capacity)).astype(jnp.int32)
        for part in range(BLOCK // LANES):
            at_line = f * (span // LANES) + at // LANES + part
            tgt_ref[at_line : at_line + 1, :] = place[:, part * LANES : (part + 1) * LANES]
    request = jnp.maximum(request, 128.0)
    power = jnp.floor(jnp.log2(request) + 0.002)
    asked = (power - 7.0) * 128.0 + jnp.round(request * jnp.exp2(7.0 - power)) - 128.0
    req_ref[:, :capacity] = asked.astype(jnp.int32)
    req_ref[:, capacity:] = jnp.zeros((owners, LANES - capacity), jnp.int32)
    copies[3].wait()


def widen(dst_ref, src_ref, step=256):
    def convert(i, _):
        at = pl.multiple_of(i * step, step)
        dst_ref[pl.ds(at + PAD, step), :] = src_ref[pl.ds(at, step), :].astype(jnp.float32)
        return 0

    lax.fori_loop(0, src_ref.shape[0] // step, convert, 0)


def gather_rows(wide_ref, index_of, count):
    sublane = lax.broadcasted_iota(jnp.int32, (8, wide_ref.shape[1]), 0)
    tiles = []
    for base in range(0, count, 8):
        tile = wide_ref[pl.ds(index_of(base) + PAD, 8), :]
        for r in range(1, 8):
            tile = jnp.where(sublane == r, wide_ref[pl.ds(index_of(base + r) + (PAD - r), 8), :], tile)
        tiles.append(tile)
    return jnp.concatenate(tiles, axis=0)


def in_windows(source_ref, buffers, sems, body):
    lines = buffers[0].shape[0]
    windows = source_ref.shape[0] // lines
    depth = len(buffers)

    def fetch(w, b):
        at = pl.multiple_of(w * lines, lines)
        return pltpu.make_async_copy(source_ref.at[pl.ds(at, lines)], buffers[b], sems.at[b])

    for b in range(depth):
        fetch(b, b).start()

    def turn(k, _):
        for b in range(depth):
            w = k * depth + b
            fetch(w, b).wait()
            body(w, buffers[b])

            @pl.when(w + depth < windows)
            def _():
                fetch(w + depth, b).start()

        return 0

    return lambda: lax.fori_loop(0, windows // depth, turn, 0)


def lookup_kernel(inc_ref, tab_ref, out_ref, wide_ref, sems, *buffers):
    capacity = out_ref.shape[1]

    def window(w, index_ref):
        lines = index_ref.shape[0]
        for d in range(lines):
            for g in range(0, capacity, GROUP):
                rows = gather_rows(wide_ref, lambda r: index_ref[d, g + r], GROUP)
                out_ref[w * lines + d, g : g + GROUP, :] = rows.astype(out_ref.dtype)

    run = in_windows(inc_ref, buffers, sems, window)
    widen(wide_ref, tab_ref)
    run()


def place_kernel(len_hbm, tgt_ref, ret_ref, out_hbm, len_ref, wide, out_ref, out_sem, len_sem, sems, *buffers):
    slots = ret_ref.shape[0]
    feats, span = out_ref.shape[:2]
    lengths_copy = pltpu.make_async_copy(len_hbm, len_ref, len_sem)
    lengths_copy.start()

    def features(w, index_ref):
        lines = span // LANES
        for k in range(index_ref.shape[0] // lines):
            feature(w * (index_ref.shape[0] // lines) + k, k * lines, index_ref)

    def feature(f, line, index_ref):
        used = len_ref[0, f]
        for at in range(0, span, WINDOW):

            @pl.when(used > at)
            def _():
                for g in range(at, at + WINDOW, GROUP):
                    rows = gather_rows(
                        wide,
                        lambda r: index_ref[line + (g + r) // LANES, (g + r) % LANES],
                        GROUP,
                    )
                    out_ref[f, g : g + GROUP, :] = rows.astype(out_ref.dtype)

        pltpu.make_async_copy(out_ref.at[f], out_hbm.at[f], out_sem).start()

    run = in_windows(tgt_ref, buffers, sems, features)
    widen(wide, ret_ref)
    wide[PAD + slots :, :] = jnp.zeros((wide.shape[0] - slots - PAD, wide.shape[1]), jnp.float32)

    def clear(f, _):
        out_ref[f] = jnp.zeros(out_ref.shape[1:], out_ref.dtype)
        return 0

    lax.fori_loop(0, feats, clear, 0)
    lengths_copy.wait()
    run()
    pltpu.make_async_copy(out_ref, out_hbm, out_sem).wait()


def on_device(lengths, id_lists, feature_slots, embedding_table):
    num_users, num_feats, list_span = id_lists.shape
    rows, row_width = embedding_table.shape
    owners = lax.axis_size("ep") * lax.axis_size("dp")
    per_owner = rows // num_feats
    slot_total = num_users * num_feats * list_span
    capacity = 5 * slot_total // (4 * owners)
    axes = ("ep", "dp")
    dtype = embedding_table.dtype
    vmem = pl.BlockSpec(memory_space=pltpu.VMEM)
    hbm = pl.BlockSpec(memory_space=pltpu.HBM)
    ids = id_lists.reshape(num_feats, list_span)

    request, targets, table = pl.pallas_call(
        functools.partial(rank_kernel, per_owner, capacity),
        out_shape=(
            pltpu.VMEM((owners, LANES), jnp.int32),
            pltpu.VMEM((slot_total // LANES, LANES), jnp.int32),
            pltpu.VMEM((rows, row_width), dtype),
        ),
        in_specs=[hbm] * 4,
        out_specs=(vmem,) * 3,
        scratch_shapes=[
            pltpu.SMEM(lengths.shape, jnp.int32),
            pltpu.SMEM(feature_slots.shape, jnp.int32),
            pltpu.VMEM(ids.shape, jnp.int32),
            pltpu.SemaphoreType.DMA((4,)),
        ],
        compiler_params=pltpu.CompilerParams(vmem_limit_bytes=16 * MIB),
        name="rank_ids",
    )(*(pltpu.with_memory_space_constraint(x, pltpu.HBM) for x in (lengths, feature_slots, ids, embedding_table)))
    incoming = lax.all_to_all(request, axes, split_axis=0, concat_axis=0, tiled=True)
    replies = pl.pallas_call(
        lookup_kernel,
        out_shape=jax.ShapeDtypeStruct((owners, capacity, row_width), dtype),
        in_specs=[vmem, vmem],
        out_specs=vmem,
        scratch_shapes=[
            pltpu.VMEM((PAD + rows + PAD, row_width), jnp.float32),
            pltpu.SemaphoreType.DMA((DEPTH,)),
        ]
        + [pltpu.SMEM((LINES, LANES), jnp.int32)] * DEPTH,
        compiler_params=pltpu.CompilerParams(vmem_limit_bytes=16 * MIB),
        name="lookup_rows",
    )(incoming, table)
    returned = lax.all_to_all(replies, axes, split_axis=0, concat_axis=0, tiled=True)
    returned = returned.reshape(owners * capacity, row_width)
    embedded = pl.pallas_call(
        place_kernel,
        out_shape=jax.ShapeDtypeStruct((num_feats, list_span, row_width), dtype),
        in_specs=[hbm, vmem, vmem],
        out_specs=hbm,
        scratch_shapes=[
            pltpu.SMEM(lengths.shape, jnp.int32),
            pltpu.VMEM((PAD + owners * capacity + 2 * PAD, row_width), jnp.float32),
            pltpu.VMEM((num_feats, list_span, row_width), dtype),
            pltpu.SemaphoreType.DMA,
            pltpu.SemaphoreType.DMA,
            pltpu.SemaphoreType.DMA((DEPTH,)),
        ]
        + [pltpu.SMEM((LINES, LANES), jnp.int32)] * DEPTH,
        compiler_params=pltpu.CompilerParams(vmem_limit_bytes=20 * MIB),
        name="place_rows",
    )(pltpu.with_memory_space_constraint(lengths, pltpu.HBM), targets, returned)
    return embedded.reshape(num_users, num_feats, list_span, row_width)


def solution(mesh):
    placed = (P(("ep", "dp"), None), P(("ep", "dp"), None, None), P(), P(("ep", "dp"), None))
    return jax.shard_map(
        on_device,
        mesh=mesh,
        in_specs=placed,
        out_specs=P(("ep", "dp"), None, None, None),
        check_vma=False,
    )
```

profile of v0, /device:TPU:1, one launch (start us, length us, event | category | flops | bytes accessed | tf_op | source)
XLA Modules:
  0.0 74.8 jit_solution(4367318207012317514)
XLA Ops:
  0.0 2.3 %rank_ids.1 = (s32[128,128]{1,0:T(8,128)S(1)}, s32[64,128]{1,0:T(8,128)S(1)}, bf16[8192,128]{1,0:T(8,128)(2,1)S(1)}) custom-call(s32[1,16]{1,0:T(1,128)} %len_hbm.3, s32[16]{0:T(128)} %slot_hbm.1, s32[16,512]{1,0:T(8,128)} %bitcast.10, bf16[8192,128]{1,0:T(8,128)(2,1)} %tab_hbm.1), custom_call_target="tpu_custom_call" | custom-call | tf_op jit(solution)/shard_map/rank_ids/pallas_call | solution.py:227
  2.3 21.2 %all_to_all.16 = s32[128,1,128]{2,1,0:T(1,128)S(1)} all-to-all(s32[128,1,128]{2,1,0:T(1,128)S(1)} %bitcast.9), channel_id=1, replica_groups=mesh['ep'=32,'dp'=4] {'ep','dp'}, dimensions={0} | all-to-all | bytes 131072 | tf_op jit(solution)/shard_map/all_to_all | solution.py:245
  23.5 6.2 %lookup_rows.1 = bf16[128,80,128]{2,1,0:T(8,128)(2,1)S(1)} custom-call(s32[128,128]{1,0:T(8,128)S(1)} %bitcast.8, bf16[8192,128]{1,0:T(8,128)(2,1)S(1)} %get-tuple-element.10.tab_ref), custom_call_target="tpu_custom_call" | custom-call | tf_op jit(solution)/shard_map/lookup_rows/pallas_call | solution.py:246
  29.7 40.4 %all_to_all.17 = bf16[128,80,128]{2,1,0:T(8,128)(2,1)S(1)} all-to-all(bf16[128,80,128]{2,1,0:T(8,128)(2,1)S(1)} %lookup_rows.1), channel_id=1, replica_groups=mesh['ep'=32,'dp'=4] {'ep','dp'}, dimensions={0} | all-to-all | bytes 5242880 | tf_op jit(solution)/shard_map/all_to_all | solution.py:259
  70.2 4.6 %place_rows.1 = bf16[16,512,128]{2,1,0:T(8,128)(2,1)} custom-call(s32[1,16]{1,0:T(1,128)} %len_hbm.3, s32[64,128]{1,0:T(8,128)S(1)} %get-tuple-element.8.tgt_ref, bf16[10240,128]{1,0:T(8,128)(2,1)S(1)} %bitcast.7), custom_call_target="tpu_custom_call" | custom-call | tf_op jit(solution)/shard_map/place_rows/pallas_call | solution.py:261
where the time goes:
time: 75.1 us; the launch traced here: 74.8 us
  blocking collectives  61.7 us (82%)
  Pallas kernels  13.1 us (17%)
    all_to_all x1, blocking collectives, on_device(): lax.all_to_all(replies, axes, split_axis=0, concat_axis=0, tiled=True)  40.4 us
    all_to_all x1, blocking collectives, on_device(): lax.all_to_all(request, axes, split_axis=0, concat_axis=0, tiled=True)  21.2 us
    pallas_call x1, Pallas kernels, on_device(): pl.pallas_call(lookup_kernel, out_shape=jax.ShapeDtypeStruct((owners, cap...  6.18 us
    pallas_call x1, Pallas kernels, on_device(): pl.pallas_call(place_kernel, out_shape=jax.ShapeDtypeStruct((num_feats, l...  4.6 us
    pallas_call x1, Pallas kernels, on_device(): pl.pallas_call(functools.partial(rank_kernel, per_owner, capacity), out_s...  2.32 us

commit v1 on v0

--- a/solution.py
+++ b/solution.py
@@ -14,6 +14,7 @@
 PAD = 8
 DEPTH = 2
 LINES = 16
+FEW = 48
 MIB = 2**20
 
 
@@ -104,7 +105,8 @@
     power = jnp.floor(jnp.log2(request) + 0.002)
     asked = (power - 7.0) * 128.0 + jnp.round(request * jnp.exp2(7.0 - power)) - 128.0
     req_ref[:, :capacity] = asked.astype(jnp.int32)
-    req_ref[:, capacity:] = jnp.zeros((owners, LANES - capacity), jnp.int32)
+    count = jnp.concatenate([x.astype(jnp.float32) for x in offset], axis=0)
+    req_ref[:, capacity:] = count[:, capacity:].astype(jnp.int32)
     copies[3].wait()
 
 
@@ -158,12 +160,25 @@
 def lookup_kernel(inc_ref, tab_ref, out_ref, wide_ref, sems, *buffers):
     capacity = out_ref.shape[1]
 
-    def window(w, index_ref):
+    def fill(w, index_ref, ranks):
         lines = index_ref.shape[0]
         for d in range(lines):
-            for g in range(0, capacity, GROUP):
+            for g in range(0, ranks, GROUP):
                 rows = gather_rows(wide_ref, lambda r: index_ref[d, g + r], GROUP)
                 out_ref[w * lines + d, g : g + GROUP, :] = rows.astype(out_ref.dtype)
+
+    def window(w, index_ref):
+        most = functools.reduce(
+            jnp.maximum, [index_ref[d, capacity] for d in range(index_ref.shape[0])]
+        )
+
+        @pl.when(most <= FEW)
+        def _():
+            fill(w, index_ref, FEW)
+
+        @pl.when(most > FEW)
+        def _():
+            fill(w, index_ref, capacity)
 
     run = in_windows(inc_ref, buffers, sems, window)
     widen(wide_ref, tab_ref)

time: 75.1 us -> 74 us (0.985)
  Pallas kernels: 13.1 us -> 12.1 us
    pallas_call x1, Pallas kernels: 6.18 us -> 4.92 us  [on_device(): pl.pallas_call(lookup_kernel, out_shape=jax.ShapeDtypeStruct((owners, cap...]
where the time goes in v1:
time: 74 us; the launch traced here: 74.1 us
  blocking collectives  61.9 us (84%)
  Pallas kernels  12.1 us (16%)
    all_to_all x1, blocking collectives, on_device(): lax.all_to_all(replies, axes, split_axis=0, concat_axis=0, tiled=True)  40.7 us
    all_to_all x1, blocking collectives, on_device(): lax.all_to_all(request, axes, split_axis=0, concat_axis=0, tiled=True)  21.2 us
    pallas_call x1, Pallas kernels, on_device(): pl.pallas_call(lookup_kernel, out_shape=jax.ShapeDtypeStruct((owners, cap...  4.92 us
    pallas_call x1, Pallas kernels, on_device(): pl.pallas_call(place_kernel, out_shape=jax.ShapeDtypeStruct((num_feats, l...  4.88 us
    pallas_call x1, Pallas kernels, on_device(): pl.pallas_call(functools.partial(rank_kernel, per_owner, capacity), out_s...  2.32 us

profile of v1, /device:TPU:1, one launch (start us, length us, event | category | flops | bytes accessed | tf_op | source)
XLA Modules:
  0.0 74.1 jit_solution(12574222117438024990)
XLA Ops:
  0.0 2.3 %rank_ids.1 = (s32[128,128]{1,0:T(8,128)S(1)}, s32[64,128]{1,0:T(8,128)S(1)}, bf16[8192,128]{1,0:T(8,128)(2,1)S(1)}) custom-call(s32[1,16]{1,0:T(1,128)} %len_hbm.3, s32[16]{0:T(128)} %slot_hbm.1, s32[16,512]{1,0:T(8,128)} %bitcast.10, bf16[8192,128]{1,0:T(8,128)(2,1)} %tab_hbm.1), custom_call_target="tpu_custom_call" | custom-call | tf_op jit(solution)/shard_map/rank_ids/pallas_call | solution.py:242
  2.3 21.2 %all_to_all.16 = s32[128,1,128]{2,1,0:T(1,128)S(1)} all-to-all(s32[128,1,128]{2,1,0:T(1,128)S(1)} %bitcast.9), channel_id=1, replica_groups=mesh['ep'=32,'dp'=4] {'ep','dp'}, dimensions={0} | all-to-all | bytes 131072 | tf_op jit(solution)/shard_map/all_to_all | solution.py:260
  23.5 4.9 %lookup_rows.1 = bf16[128,80,128]{2,1,0:T(8,128)(2,1)S(1)} custom-call(s32[128,128]{1,0:T(8,128)S(1)} %bitcast.8, bf16[8192,128]{1,0:T(8,128)(2,1)S(1)} %get-tuple-element.10.tab_ref), custom_call_target="tpu_custom_call" | custom-call | tf_op jit(solution)/shard_map/lookup_rows/pallas_call | solution.py:261
  28.5 40.7 %all_to_all.17 = bf16[128,80,128]{2,1,0:T(8,128)(2,1)S(1)} all-to-all(bf16[128,80,128]{2,1,0:T(8,128)(2,1)S(1)} %lookup_rows.1), channel_id=1, replica_groups=mesh['ep'=32,'dp'=4] {'ep','dp'}, dimensions={0} | all-to-all | bytes 5242880 | tf_op jit(solution)/shard_map/all_to_all | solution.py:274
  69.2 4.9 %place_rows.1 = bf16[16,512,128]{2,1,0:T(8,128)(2,1)} custom-call(s32[1,16]{1,0:T(1,128)} %len_hbm.3, s32[64,128]{1,0:T(8,128)S(1)} %get-tuple-element.8.tgt_ref, bf16[10240,128]{1,0:T(8,128)(2,1)S(1)} %bitcast.7), custom_call_target="tpu_custom_call" | custom-call | tf_op jit(solution)/shard_map/place_rows/pallas_call | solution.py:276

commit v2 on v1

--- a/solution.py
+++ b/solution.py
@@ -14,7 +14,7 @@
 PAD = 8
 DEPTH = 2
 LINES = 16
-FEW = 48
+TIERS = (48, 64)
 MIB = 2**20
 
 
@@ -172,13 +172,14 @@
             jnp.maximum, [index_ref[d, capacity] for d in range(index_ref.shape[0])]
         )
 
-        @pl.when(most <= FEW)
-        def _():
-            fill(w, index_ref, FEW)
-
-        @pl.when(most > FEW)
-        def _():
-            fill(w, index_ref, capacity)
+        floor = -1
+        for ranks in TIERS + (capacity,):
+
+            @pl.when((most > floor) & ((most <= ranks) | (ranks == capacity)))
+            def _():
+                fill(w, index_ref, ranks)
+
+            floor = ranks
 
     run = in_windows(inc_ref, buffers, sems, window)
     widen(wide_ref, tab_ref)

time: 74 us -> 74.1 us (level)
  no operation moved by 1% of the time
where the time goes in v2:
time: 74.1 us; the launch traced here: 74.3 us
  blocking collectives  62.2 us (84%)
  Pallas kernels  12.1 us (16%)
    all_to_all x1, blocking collectives, on_device(): lax.all_to_all(replies, axes, split_axis=0, concat_axis=0, tiled=True)  41 us
    all_to_all x1, blocking collectives, on_device(): lax.all_to_all(request, axes, split_axis=0, concat_axis=0, tiled=True)  21.2 us
    pallas_call x1, Pallas kernels, on_device(): pl.pallas_call(lookup_kernel, out_shape=jax.ShapeDtypeStruct((owners, cap...  5.08 us
    pallas_call x1, Pallas kernels, on_device(): pl.pallas_call(place_kernel, out_shape=jax.ShapeDtypeStruct((num_feats, l...  4.68 us
    pallas_call x1, Pallas kernels, on_device(): pl.pallas_call(functools.partial(rank_kernel, per_owner, capacity), out_s...  2.32 us

profile of v2, /device:TPU:1, one launch (start us, length us, event | category | flops | bytes accessed | tf_op | source)
XLA Modules:
  0.0 74.3 jit_solution(10373514779516539840)
XLA Ops:
  0.0 2.3 %rank_ids.1 = (s32[128,128]{1,0:T(8,128)S(1)}, s32[64,128]{1,0:T(8,128)S(1)}, bf16[8192,128]{1,0:T(8,128)(2,1)S(1)}) custom-call(s32[1,16]{1,0:T(1,128)} %len_hbm.3, s32[16]{0:T(128)} %slot_hbm.1, s32[16,512]{1,0:T(8,128)} %bitcast.10, bf16[8192,128]{1,0:T(8,128)(2,1)} %tab_hbm.1), custom_call_target="tpu_custom_call" | custom-call | tf_op jit(solution)/shard_map/rank_ids/pallas_call | solution.py:243
  2.3 21.2 %all_to_all.16 = s32[128,1,128]{2,1,0:T(1,128)S(1)} all-to-all(s32[128,1,128]{2,1,0:T(1,128)S(1)} %bitcast.9), channel_id=1, replica_groups=mesh['ep'=32,'dp'=4] {'ep','dp'}, dimensions={0} | all-to-all | bytes 131072 | tf_op jit(solution)/shard_map/all_to_all | solution.py:261
  23.5 5.1 %lookup_rows.1 = bf16[128,80,128]{2,1,0:T(8,128)(2,1)S(1)} custom-call(s32[128,128]{1,0:T(8,128)S(1)} %bitcast.8, bf16[8192,128]{1,0:T(8,128)(2,1)S(1)} %get-tuple-element.10.tab_ref), custom_call_target="tpu_custom_call" | custom-call | tf_op jit(solution)/shard_map/lookup_rows/pallas_call | solution.py:262
  28.6 41.0 %all_to_all.17 = bf16[128,80,128]{2,1,0:T(8,128)(2,1)S(1)} all-to-all(bf16[128,80,128]{2,1,0:T(8,128)(2,1)S(1)} %lookup_rows.1), channel_id=1, replica_groups=mesh['ep'=32,'dp'=4] {'ep','dp'}, dimensions={0} | all-to-all | bytes 5242880 | tf_op jit(solution)/shard_map/all_to_all | solution.py:275
  69.6 4.7 %place_rows.1 = bf16[16,512,128]{2,1,0:T(8,128)(2,1)} custom-call(s32[1,16]{1,0:T(1,128)} %len_hbm.3, s32[64,128]{1,0:T(8,128)S(1)} %get-tuple-element.8.tgt_ref, bf16[10240,128]{1,0:T(8,128)(2,1)S(1)} %bitcast.7), custom_call_target="tpu_custom_call" | custom-call | tf_op jit(solution)/shard_map/place_rows/pallas_call | solution.py:277

commit v3 on v1

--- a/solution.py
+++ b/solution.py
@@ -157,7 +157,7 @@
     return lambda: lax.fori_loop(0, windows // depth, turn, 0)
 
 
-def lookup_kernel(inc_ref, tab_ref, out_ref, wide_ref, sems, *buffers):
+def lookup_kernel(inc_ref, tab_ref, out_ref, wide_ref, peak_ref, peaks, peak_sem, sems, *buffers):
     capacity = out_ref.shape[1]
 
     def fill(w, index_ref, ranks):
@@ -168,9 +168,7 @@
                 out_ref[w * lines + d, g : g + GROUP, :] = rows.astype(out_ref.dtype)
 
     def window(w, index_ref):
-        most = functools.reduce(
-            jnp.maximum, [index_ref[d, capacity] for d in range(index_ref.shape[0])]
-        )
+        most = peaks[w, capacity]
 
         @pl.when(most <= FEW)
         def _():
@@ -181,7 +179,15 @@
             fill(w, index_ref, capacity)
 
     run = in_windows(inc_ref, buffers, sems, window)
+    lines = buffers[0].shape[0]
+    for w in range(peak_ref.shape[0]):
+        peak_ref[w : w + 1, :] = jnp.max(
+            inc_ref[w * lines : (w + 1) * lines, :], axis=0, keepdims=True
+        )
+    peaks_copy = pltpu.make_async_copy(peak_ref, peaks, peak_sem)
+    peaks_copy.start()
     widen(wide_ref, tab_ref)
+    peaks_copy.wait()
     run()
 
 
@@ -265,6 +271,9 @@
         out_specs=vmem,
         scratch_shapes=[
             pltpu.VMEM((PAD + rows + PAD, row_width), jnp.float32),
+            pltpu.VMEM((owners // LINES, LANES), jnp.int32),
+            pltpu.SMEM((owners // LINES, LANES), jnp.int32),
+            pltpu.SemaphoreType.DMA,
             pltpu.SemaphoreType.DMA((DEPTH,)),
         ]
         + [pltpu.SMEM((LINES, LANES), jnp.int32)] * DEPTH,

time: 74 us -> 74.7 us (level)
  no operation moved by 1% of the time
where the time goes in v3:
time: 74.7 us; the launch traced here: 74.8 us
  blocking collectives  62.1 us (83%)
  Pallas kernels  12.6 us (17%)
    all_to_all x1, blocking collectives, on_device(): lax.all_to_all(replies, axes, split_axis=0, concat_axis=0, tiled=True)  40.9 us
    all_to_all x1, blocking collectives, on_device(): lax.all_to_all(request, axes, split_axis=0, concat_axis=0, tiled=True)  21.2 us
    pallas_call x1, Pallas kernels, on_device(): pl.pallas_call(lookup_kernel, out_shape=jax.ShapeDtypeStruct((owners, cap...  5.55 us
    pallas_call x1, Pallas kernels, on_device(): pl.pallas_call(place_kernel, out_shape=jax.ShapeDtypeStruct((num_feats, l...  4.75 us
    pallas_call x1, Pallas kernels, on_device(): pl.pallas_call(functools.partial(rank_kernel, per_owner, capacity), out_s...  2.32 us

profile of v3, /device:TPU:1, one launch (start us, length us, event | category | flops | bytes accessed | tf_op | source)
XLA Modules:
  0.0 74.8 jit_solution(1398803186291198576)
XLA Ops:
  0.0 2.3 %rank_ids.1 = (s32[128,128]{1,0:T(8,128)S(1)}, s32[64,128]{1,0:T(8,128)S(1)}, bf16[8192,128]{1,0:T(8,128)(2,1)S(1)}) custom-call(s32[1,16]{1,0:T(1,128)} %len_hbm.3, s32[16]{0:T(128)} %slot_hbm.1, s32[16,512]{1,0:T(8,128)} %bitcast.10, bf16[8192,128]{1,0:T(8,128)(2,1)} %tab_hbm.1), custom_call_target="tpu_custom_call" | custom-call | tf_op jit(solution)/shard_map/rank_ids/pallas_call | solution.py:248
  2.3 21.2 %all_to_all.16 = s32[128,1,128]{2,1,0:T(1,128)S(1)} all-to-all(s32[128,1,128]{2,1,0:T(1,128)S(1)} %bitcast.9), channel_id=1, replica_groups=mesh['ep'=32,'dp'=4] {'ep','dp'}, dimensions={0} | all-to-all | bytes 131072 | tf_op jit(solution)/shard_map/all_to_all | solution.py:266
  23.5 5.6 %lookup_rows.1 = bf16[128,80,128]{2,1,0:T(8,128)(2,1)S(1)} custom-call(s32[128,128]{1,0:T(8,128)S(1)} %bitcast.8, bf16[8192,128]{1,0:T(8,128)(2,1)S(1)} %get-tuple-element.10.tab_ref), custom_call_target="tpu_custom_call" | custom-call | tf_op jit(solution)/shard_map/lookup_rows/pallas_call | solution.py:267
  29.1 40.9 %all_to_all.17 = bf16[128,80,128]{2,1,0:T(8,128)(2,1)S(1)} all-to-all(bf16[128,80,128]{2,1,0:T(8,128)(2,1)S(1)} %lookup_rows.1), channel_id=1, replica_groups=mesh['ep'=32,'dp'=4] {'ep','dp'}, dimensions={0} | all-to-all | bytes 5242880 | tf_op jit(solution)/shard_map/all_to_all | solution.py:283
  70.0 4.7 %place_rows.1 = bf16[16,512,128]{2,1,0:T(8,128)(2,1)} custom-call(s32[1,16]{1,0:T(1,128)} %len_hbm.3, s32[64,128]{1,0:T(8,128)S(1)} %get-tuple-element.8.tgt_ref, bf16[10240,128]{1,0:T(8,128)(2,1)S(1)} %bitcast.7), custom_call_target="tpu_custom_call" | custom-call | tf_op jit(solution)/shard_map/place_rows/pallas_call | solution.py:285

commit v4 on v3

--- a/solution.py
+++ b/solution.py
@@ -14,6 +14,8 @@
 PAD = 8
 DEPTH = 2
 LINES = 16
+ASK_DEPTH = 4
+ASK_LINES = 8
 FEW = 48
 MIB = 2**20
 
@@ -271,12 +273,12 @@
         out_specs=vmem,
         scratch_shapes=[
             pltpu.VMEM((PAD + rows + PAD, row_width), jnp.float32),
-            pltpu.VMEM((owners // LINES, LANES), jnp.int32),
-            pltpu.SMEM((owners // LINES, LANES), jnp.int32),
+            pltpu.VMEM((owners // ASK_LINES, LANES), jnp.int32),
+            pltpu.SMEM((owners // ASK_LINES, LANES), jnp.int32),
             pltpu.SemaphoreType.DMA,
-            pltpu.SemaphoreType.DMA((DEPTH,)),
+            pltpu.SemaphoreType.DMA((ASK_DEPTH,)),
         ]
-        + [pltpu.SMEM((LINES, LANES), jnp.int32)] * DEPTH,
+        + [pltpu.SMEM((ASK_LINES, LANES), jnp.int32)] * ASK_DEPTH,
         compiler_params=pltpu.CompilerParams(vmem_limit_bytes=16 * MIB),
         name="lookup_rows",
     )(incoming, table)

time: 74.7 us -> 74 us (level)
  Pallas kernels: 12.6 us -> 11.4 us
    pallas_call x1, Pallas kernels: 5.55 us -> 4.79 us  [on_device(): pl.pallas_call(lookup_kernel, out_shape=jax.ShapeDtypeStruct((owners, cap...]
where the time goes in v4:
time: 74 us; the launch traced here: 73.5 us
  blocking collectives  62.1 us (84%)
  Pallas kernels  11.4 us (15%)
    all_to_all x1, blocking collectives, on_device(): lax.all_to_all(replies, axes, split_axis=0, concat_axis=0, tiled=True)  40.9 us
    all_to_all x1, blocking collectives, on_device(): lax.all_to_all(request, axes, split_axis=0, concat_axis=0, tiled=True)  21.2 us
    pallas_call x1, Pallas kernels, on_device(): pl.pallas_call(lookup_kernel, out_shape=jax.ShapeDtypeStruct((owners, cap...  4.79 us
    pallas_call x1, Pallas kernels, on_device(): pl.pallas_call(place_kernel, out_shape=jax.ShapeDtypeStruct((num_feats, l...  4.26 us
    pallas_call x1, Pallas kernels, on_device(): pl.pallas_call(functools.partial(rank_kernel, per_owner, capacity), out_s...  2.32 us

profile of v4, /device:TPU:1, one launch (start us, length us, event | category | flops | bytes accessed | tf_op | source)
XLA Modules:
  0.0 73.5 jit_solution(17059242892538868986)
XLA Ops:
  0.0 2.3 %rank_ids.1 = (s32[128,128]{1,0:T(8,128)S(1)}, s32[64,128]{1,0:T(8,128)S(1)}, bf16[8192,128]{1,0:T(8,128)(2,1)S(1)}) custom-call(s32[1,16]{1,0:T(1,128)} %len_hbm.3, s32[16]{0:T(128)} %slot_hbm.1, s32[16,512]{1,0:T(8,128)} %bitcast.10, bf16[8192,128]{1,0:T(8,128)(2,1)} %tab_hbm.1), custom_call_target="tpu_custom_call" | custom-call | tf_op jit(solution)/shard_map/rank_ids/pallas_call | solution.py:250
  2.3 21.2 %all_to_all.16 = s32[128,1,128]{2,1,0:T(1,128)S(1)} all-to-all(s32[128,1,128]{2,1,0:T(1,128)S(1)} %bitcast.9), channel_id=1, replica_groups=mesh['ep'=32,'dp'=4] {'ep','dp'}, dimensions={0} | all-to-all | bytes 131072 | tf_op jit(solution)/shard_map/all_to_all | solution.py:268
  23.5 4.8 %lookup_rows.1 = bf16[128,80,128]{2,1,0:T(8,128)(2,1)S(1)} custom-call(s32[128,128]{1,0:T(8,128)S(1)} %bitcast.8, bf16[8192,128]{1,0:T(8,128)(2,1)S(1)} %get-tuple-element.10.tab_ref), custom_call_target="tpu_custom_call" | custom-call | tf_op jit(solution)/shard_map/lookup_rows/pallas_call | solution.py:269
  28.3 40.9 %all_to_all.17 = bf16[128,80,128]{2,1,0:T(8,128)(2,1)S(1)} all-to-all(bf16[128,80,128]{2,1,0:T(8,128)(2,1)S(1)} %lookup_rows.1), channel_id=1, replica_groups=mesh['ep'=32,'dp'=4] {'ep','dp'}, dimensions={0} | all-to-all | bytes 5242880 | tf_op jit(solution)/shard_map/all_to_all | solution.py:285
  69.2 4.3 %place_rows.1 = bf16[16,512,128]{2,1,0:T(8,128)(2,1)} custom-call(s32[1,16]{1,0:T(1,128)} %len_hbm.3, s32[64,128]{1,0:T(8,128)S(1)} %get-tuple-element.8.tgt_ref, bf16[10240,128]{1,0:T(8,128)(2,1)S(1)} %bitcast.7), custom_call_target="tpu_custom_call" | custom-call | tf_op jit(solution)/shard_map/place_rows/pallas_call | solution.py:287
